TPU v7x, 128 devices: a whole 4x4x4 slice. The times are simulated.
128 devices in a mesh: depth: 4 (over z), col: 4 (over y), row: 8 (over x, core).
Axes of the slice: x: 4, y: 4, z: 4, core: 2. Of those that a mesh axis runs over, the one named last changes fastest.
Arguments:
- weight: bfloat16 [12288, 12288], P(('row', 'depth'), 'col')
- rhs_stack: bfloat16 [3, 12288, 8192], P(None, ('row', 'depth'), 'col')
Outputs:
- output: bfloat16 [3, 12288, 8192], P(None, ('row', 'depth'), 'col')
All inputs are finite; a program needn't handle non-finite values.
Results may differ from a plain program's by a relative error of at most 0.001.
Values are sent between devices in bfloat16 or wider.
A program may use at most 1 GiB of HBM per device.

v0:
```python
import jax
import jax.numpy as jnp
from jax import lax
from jax.sharding import PartitionSpec as P

ALL_AXES = ("depth", "col", "row")


def solution(mesh):
    depth_size = mesh.shape["depth"]
    col_size = mesh.shape["col"]
    row_size = mesh.shape["row"]
    group_size = row_size // col_size
    layer_steps = row_size // depth_size
    all_coords = [(layer_idx, col_idx, row_idx) for layer_idx in range(depth_size) for col_idx in range(col_size) for row_idx in range(row_size)]

    def linear_index(coords):
        layer_idx, col_idx, row_idx = coords
        return (layer_idx * col_size + col_idx) * row_size + row_idx

    def a_source(coords, extra):
        layer_idx, col_idx, row_idx = coords
        block_shift = (row_idx + layer_idx * layer_steps) // group_size
        return linear_index((layer_idx, (col_idx + block_shift + extra) % col_size, row_idx))

    def x_source(coords, piece_idx):
        layer_idx, col_idx, row_idx = coords
        src_row = (row_idx + col_idx * group_size + piece_idx + layer_idx * layer_steps) % row_size
        return linear_index((layer_idx, col_idx, src_row))

    perm_a_near = [(a_source(coords, 0), linear_index(coords)) for coords in all_coords]
    perm_a_next = [(a_source(coords, 1), linear_index(coords)) for coords in all_coords]
    perm_x_pieces = [[(x_source(coords, piece_idx), linear_index(coords)) for coords in all_coords] for piece_idx in range(group_size)]
    perm_col_shift = [(col_idx, (col_idx - 1) % col_size) for col_idx in range(col_size)]
    perm_row_shift = [(row_idx, (row_idx - 1) % row_size) for row_idx in range(row_size)]

    def local_product(w_local, x_local):
        rhs_count = x_local.shape[0]
        slice_rows = x_local.shape[1]
        block_cols = x_local.shape[2] // group_size
        w_layer = lax.all_gather(w_local, "depth", axis=0, tiled=True)
        block_rows = w_layer.shape[0]
        x_split = jnp.transpose(x_local.reshape(rhs_count, slice_rows, group_size, block_cols), (2, 1, 0, 3))
        x_layer = lax.all_gather(x_split, "depth", axis=1, tiled=True)
        layer_idx = lax.axis_index("depth")
        row_idx = lax.axis_index("row")
        offset = (row_idx + layer_idx * layer_steps) % group_size
        w_near = lax.ppermute(w_layer, ALL_AXES, perm_a_near)
        if group_size > 1:
            w_next = lax.ppermute(w_layer, ALL_AXES, perm_a_next)
            w_pair = jnp.concatenate([w_near, w_next], axis=1).reshape(block_rows, 2 * group_size, block_rows)
            w_start = lax.dynamic_slice_in_dim(w_pair, offset, group_size, axis=1)
        else:
            w_start = w_near.reshape(block_rows, 1, block_rows)
        w_blocks = jnp.transpose(w_start, (1, 0, 2))
        x_blocks = jnp.stack([lax.ppermute(x_layer[piece_idx], ALL_AXES, perm_x_pieces[piece_idx]) for piece_idx in range(group_size)], axis=0)
        partial_sum = jnp.einsum("tik,tkrm->tirm", w_blocks, x_blocks, preferred_element_type=jnp.float32)
        for step_idx in range(1, layer_steps):
            w_recv = lax.ppermute(w_blocks[0], "col", perm_col_shift)
            w_blocks = jnp.concatenate([w_blocks[1:], w_recv[None]], axis=0)
            x_blocks = lax.ppermute(x_blocks, "row", perm_row_shift)
            partial_sum = partial_sum + jnp.einsum("tik,tkrm->tirm", w_blocks, x_blocks, preferred_element_type=jnp.float32)
        reduced = lax.psum_scatter(partial_sum, "depth", scatter_dimension=1, tiled=True)
        rounded = reduced.astype(jnp.bfloat16)
        return jnp.transpose(rounded, (2, 1, 0, 3)).reshape(rhs_count, slice_rows, group_size * block_cols)

    return jax.shard_map(local_product, mesh=mesh, in_specs=(P(("row", "depth"), "col"), P(None, ("row", "depth"), "col")), out_specs=P(None, ("row", "depth"), "col"), check_vma=False)
```

profile of v0, /device:TPU:0, one launch (start us, length us, event | category | flops | bytes accessed | tf_op | source)
XLA Modules:
  0.0 1608.3 jit_solution(6713140602617904604)
XLA Ops:
  6.5 0.0 all-gather.5.cloned.1.call-start
  6.5 6.6 copy.5
  13.2 0.0 copy-start.2
  13.2 6.8 copy.6
  20.0 0.0 all-gather.5.cloned.1.call-update
  20.0 0.0 all-gather.3.cloned.1.call-start
  20.0 0.0 copy-done.2
  20.0 2.4 copy.3
  22.5 0.0 all-gather.3.cloned.1.call-update
  22.5 0.0 reduce-scatter.2.cloned.1.call-start
  22.6 173.2 %all-gather.5.cloned.1.call-done = bf16[2,1536,3,1024]{3,1,2,0:T(8,128)(2,1)} async-done(((bf16[2,384,3,1024]{3,1,2,0:T(8,128)(2,1)}), bf16[2,1536,3,1024]{3,1,2,0:T(8,128)(2,1)}) %all-gather.5.cloned.1.call-update) | async-done | bytes 18874384 | tf_op jit(solution)/shard_map/all_gather | solution.py:44
  195.8 7.9 slice_bitcast_fusion.1
  203.6 1.3 collective-permute-start.2
  204.9 1.9 collective-permute-start.3
  206.9 0.0 collective-permute-done.2
  206.9 0.0 copy-start
  206.9 102.2 %collective-permute-done.3 = bf16[1536,3,1024]{2,0,1:T(8,128)(2,1)S(1)} collective-permute-done((bf16[1536,3,1024]{2,0,1:T(8,128)(2,1)S(1)}, bf16[1536,3,1024]{2,0,1:T(8,128)(2,1)S(1)}, u32[]{:S(2)}, u32[]{:S(2)}) %collective-permute-start.3) | collective-permute-done | bytes 9437216 | tf_op jit(solution)/shard_map/ppermute | solution.py:56
  309.0 0.0 copy-start.1
  309.0 9.6 pad_maximum_fusion.1
  318.6 0.0 copy-done
  318.6 0.0 copy-done.1
  318.6 3.1 collective-permute-start.5
  321.8 0.0 all-gather.3.cloned.1.call-done
  321.8 204.8 %collective-permute-start.1 = (bf16[1536,3072]{0,1:T(8,128)(2,1)}, bf16[1536,3072]{0,1:T(8,128)(2,1)}, u32[]{:S(2)}, u32[]{:S(2)}) collective-permute-start(bf16[1536,3072]{0,1:T(8,128)(2,1)} %all-gather.3.cloned.1.call-done), channel_id=1, source_target_pairs={{8,0},{9,1},{18,2},{19,3},{28,4},{29,5},{6,6},{7,7},{16,8},{17,9},... | collective-permute-start | bytes 28311560 | tf_op jit(solution)/shard_map/ppermute | solution.py:50
  526.6 72.0 %collective-permute-start = (bf16[1536,3072]{0,1:T(8,128)(2,1)}, bf16[1536,3072]{0,1:T(8,128)(2,1)}, u32[]{:S(2)}, u32[]{:S(2)}) collective-permute-start(bf16[1536,3072]{0,1:T(8,128)(2,1)} %all-gather.3.cloned.1.call-done), channel_id=1, source_target_pairs={{0,0},{1,1},{10,2},{11,3},{20,4},{21,5},{30,6},{31,7},{8,8},{9,9},... | collective-permute-start | bytes 28311560 | tf_op jit(solution)/shard_map/ppermute | solution.py:48
  598.5 230.0 %collective-permute-done.1 = bf16[1536,3072]{0,1:T(8,128)(2,1)} collective-permute-done((bf16[1536,3072]{0,1:T(8,128)(2,1)}, bf16[1536,3072]{0,1:T(8,128)(2,1)}, u32[]{:S(2)}, u32[]{:S(2)}) %collective-permute-start.1) | collective-permute-done | bytes 9437216 | tf_op jit(solution)/shard_map/ppermute | solution.py:50
  828.6 0.0 collective-permute-done
  828.6 20.6 %pad_maximum_fusion = bf16[1536,6144]{0,1:T(8,128)(2,1)} fusion(bf16[1536,3072]{0,1:T(8,128)(2,1)} %collective-permute-done.1, bf16[1536,3072]{0,1:T(8,128)(2,1)} %collective-permute-done), kind=kLoop, calls=%fused_computation.1 | loop fusion | flops 37748736 | bytes 37748736 | tf_op jit(solution)/shard_map/concatenate | solution.py:51
  849.2 8.0 constant_dynamic-slice_fusion
  857.2 12.6 copy.11
  869.8 6.6 fusion.5
  876.3 2.4 collective-permute-start.4
  878.7 100.3 %collective-permute-done.4 = bf16[1536,1536]{1,0:T(8,128)(2,1)} collective-permute-done((bf16[1536,1536]{1,0:T(8,128)(2,1)}, bf16[1536,1536]{1,0:T(8,128)(2,1)}, u32[]{:S(2)}, u32[]{:S(2)}) %collective-permute-start.4) | collective-permute-done | bytes 4718624 | tf_op jit(solution)/shard_map/ppermute | solution.py:59
  979.0 0.0 collective-permute-done.5
  979.0 36.7 %fusion = f32[2,1536,3,1024]{3,1,2,0:T(8,128)} fusion(bf16[2,1536,3,1024]{3,1,2,0:T(8,128)(2,1)} %collective-permute-done.5, bf16[1,1536,1536]{2,1,0:T(8,128)(2,1)} %bitcast.11, bf16[1,1536,1536]{2,1,0:T(8,128)(2,1)S(1)} %get-tuple-element.7), kind=kOutput, calls=%fused_computation.6 | convolution fusion | flops 29009903616 | bytes 66060288 | tf_op jit(solution)/shard_map/tik,tkrm->tirm/dot_general | solution.py:62
  1015.7 42.2 %convolution_add_fusion = f32[2,1536,3,1024]{3,1,2,0:T(8,128)} fusion(f32[2,1536,3,1024]{3,1,2,0:T(8,128)} %fusion, bf16[1536,2,1536]{2,0,1:T(8,128)(2,1)} %copy.11, bf16[1,1536,3,1024]{3,1,2,0:T(8,128)(2,1)} %bitcast.36, bf16[1,1536,3,1024]{3,1,2,0:T(8,128)(2,1)} %bitcast.34), kind=kOutput, calls=%fused_computation | convolution fusion | flops 29038215168 | bytes 103809024 | tf_op jit(solution)/shard_map/tik,tkrm->tirm/dot_general | solution.py:57
  1057.9 0.0 reduce-scatter.2.cloned.1.call-update
  1057.9 524.1 %reduce-scatter.2.cloned.1.call-done = f32[2,384,3,1024]{3,1,2,0:T(8,128)} async-done(((f32[2,1536,3,1024]{3,1,2,0:T(8,128)}), f32[2,384,3,1024]{3,1,2,0:T(8,128)}) %reduce-scatter.2.cloned.1.call-update) | async-done | bytes 9437200 | tf_op jit(solution)/shard_map/reduce_scatter | solution.py:63
  1581.9 6.6 convert_bitcast_fusion
  1588.6 6.6 copy.7
  1595.2 6.6 copy.8
Async XLA Ops:
  6.5 189.2 %all-gather.5.cloned.1.call-start = ((), (), s32[]{:S(2)}) async-start(), calls=%async_computation.2 | async-start | bytes 23592960 | tf_op jit(solution)/shard_map/all_gather | solution.py:44
  13.2 6.9 copy-start.2
  20.0 301.8 %all-gather.3.cloned.1.call-start = ((), (), s32[]{:S(2)}) async-start(), calls=%async_computation.1 | async-start | bytes 11796480 | tf_op jit(solution)/shard_map/all_gather | solution.py:41
  22.5 1559.4 %reduce-scatter.2.cloned.1.call-start = ((), (), s32[]{:S(2)}) async-start(), calls=%async_computation.3 | async-start | bytes 47185920 | tf_op jit(solution)/shard_map/reduce_scatter | solution.py:63
  203.6 3.2 collective-permute-start.2
  204.9 104.1 %collective-permute-start.3 = (bf16[1536,3,1024]{2,0,1:T(8,128)(2,1)S(1)}, bf16[1536,3,1024]{2,0,1:T(8,128)(2,1)S(1)}, u32[]{:S(2)}, u32[]{:S(2)}) collective-permute-start(bf16[1536,3,1024]{2,0,1:T(8,128)(2,1)S(1)} %get-tuple-element.6), channel_id=1, source_target_pairs={{1,0},{2,1},{3,2},{4,3},{5,4},{6,5},{7,6},{0,7},{11,8},{12,9},{13,... | collective-permute-start | bytes 28311560 | tf_op jit(solution)/shard_map/ppermute | solution.py:56
  206.9 111.8 %copy-start = (bf16[1536,3,1024]{2,0,1:T(8,128)(2,1)}, bf16[1536,3,1024]{2,0,1:T(8,128)(2,1)S(1)}, u32[]{:S(2)}) copy-start(bf16[1536,3,1024]{2,0,1:T(8,128)(2,1)S(1)} %collective-permute-done.2) | copy-start | bytes 28311556
  309.0 9.6 copy-start.1
  318.6 660.4 %collective-permute-start.5 = (bf16[2,1536,3,1024]{3,1,2,0:T(8,128)(2,1)}, bf16[2,1536,3,1024]{3,1,2,0:T(8,128)(2,1)}, u32[]{:S(2)}, u32[]{:S(2)}) collective-permute-start(bf16[2,1536,3,1024]{3,1,2,0:T(8,128)(2,1)} %pad_maximum_fusion.1), channel_id=1, source_target_pairs={{0,7},{1,0},{2,1},{3,2},{4,3},{5,4},{6,5},{7,6},{8,15},{9,8},{10,9... | collective-permute-start | bytes 56623112 | tf_op jit(solution)/shard_map/ppermute | solution.py:61
  321.8 506.8 %collective-permute-start.1 = (bf16[1536,3072]{0,1:T(8,128)(2,1)}, bf16[1536,3072]{0,1:T(8,128)(2,1)}, u32[]{:S(2)}, u32[]{:S(2)}) collective-permute-start(bf16[1536,3072]{0,1:T(8,128)(2,1)} %all-gather.3.cloned.1.call-done), channel_id=1, source_target_pairs={{8,0},{9,1},{18,2},{19,3},{28,4},{29,5},{6,6},{7,7},{16,8},{17,9},... | collective-permute-start | bytes 28311560 | tf_op jit(solution)/shard_map/ppermute | solution.py:50
  526.6 302.0 %collective-permute-start = (bf16[1536,3072]{0,1:T(8,128)(2,1)}, bf16[1536,3072]{0,1:T(8,128)(2,1)}, u32[]{:S(2)}, u32[]{:S(2)}) collective-permute-start(bf16[1536,3072]{0,1:T(8,128)(2,1)} %all-gather.3.cloned.1.call-done), channel_id=1, source_target_pairs={{0,0},{1,1},{10,2},{11,3},{20,4},{21,5},{30,6},{31,7},{8,8},{9,9},... | collective-permute-start | bytes 28311560 | tf_op jit(solution)/shard_map/ppermute | solution.py:48
  876.3 102.7 %collective-permute-start.4 = (bf16[1536,1536]{1,0:T(8,128)(2,1)}, bf16[1536,1536]{1,0:T(8,128)(2,1)}, u32[]{:S(2)}, u32[]{:S(2)}) collective-permute-start(bf16[1536,1536]{1,0:T(8,128)(2,1)} %get-tuple-element.8), channel_id=1, source_target_pairs={{0,24},{8,0},{16,8},{24,16},{1,25},{9,1},{17,9},{25,17},{2,26},{10... | collective-permute-start | bytes 14155784 | tf_op jit(solution)/shard_map/ppermute | solution.py:59
Sparse Core Ops, SparseCore 0:
  20.1 175.6 all-gather.4
  197.4 92.3 all-gather.2
  1058.0 523.8 reduce-scatter.1
where the time goes:
time: 1620 us; the launch traced here: 1610 us
  waiting for transfers between devices  1130 us (70%)
  starting transfers between devices  286 us (18%)
  matrix products  78.8 us (5%)
  local copies, waits for them, and re-layouts  64.1 us (4%)
  other arithmetic  36.8 us (2%)
    reduce_scatter x1, waiting for transfers between devices, local_product(): lax.psum_scatter(partial_sum, 'depth', scatter_dimension=1, tiled=True)  524 us
    ppermute x1, waiting for transfers between devices, local_product(): w_next = lax.ppermute(w_layer, ALL_AXES, perm_a_next)  230 us
    ppermute x1, starting transfers between devices, local_product(): w_next = lax.ppermute(w_layer, ALL_AXES, perm_a_next)  205 us
    all_gather x1, waiting for transfers between devices, local_product(): x_layer = lax.all_gather(x_split, 'depth', axis=1, tiled=True)  173 us
    ppermute x2, waiting for transfers between devices, local_product(): lax.ppermute(x_layer[piece_idx], ALL_AXES, perm_x_pieces[piece_idx])  102 us
    ppermute x1, waiting for transfers between devices, local_product(): w_recv = lax.ppermute(w_blocks[0], 'col', perm_col_shift)  100 us
    dot_general x2, matrix products, local_product(): jnp.einsum('tik,tkrm->tirm', w_blocks, x_blocks, preferred_element_type=j...  78.8 us
    ppermute x1, starting transfers between devices, local_product(): w_near = lax.ppermute(w_layer, ALL_AXES, perm_a_near)  72 us
  transfers between devices with their start and end apart: 9, of which 5 were waited for; matrix products, arithmetic and copies ran while one was open for 4% of the time, Pallas kernels for 0%

commit v1 on v0

v1 whole, which is shorter than its diff:
```python
import functools

import jax
import jax.numpy as jnp
from jax import lax
from jax.experimental import pallas as pl
from jax.experimental.pallas import tpu as pltpu
from jax.sharding import PartitionSpec as P

MESH = pl.DeviceIdType.MESH
MODES = "babababbabab"
A_PIECES = 4
SLOTS = 3
DEPTH_Q = 2
RATE = {"xp": 46.0e3, "xm": 46.0e3, "yp": 46.0e3, "ym": 46.0e3, "zl": 46.0e3, "zh": 46.0e3, "dd": 250.0e3}
LAT = {"dd": 1.5}


def make_plan(chunks, modes, unit, a_unit, half_us):
    sends = {}

    def add(name, link, size, deps, key):
        sends[name] = (link, size, frozenset(deps), key)

    need = {}
    for j in range(chunks):
        S, L = ("S", j), ("L", j)
        add(L, "zl", unit, [], j - 1)
        if modes[j] == "b":
            add(("H", j), "zh", 2 * unit, [S, L], j - 1.5)
            add(("R1", j), "xp", 4 * unit, [S, L, ("H", j)], (j, 1))
            add(("L1", j), "xm", 4 * unit, [S, L, ("H", j)], (j, 1))
            add(("R2", j), "xp", 2 * unit, [("R1", j)], (j, 0))
            add(("L2", j), "xm", 2 * unit, [("L1", j)], (j, 0))
            got = {0: [S, L, ("H", j)], -1: [("R1", j)], 1: [("L1", j)], 2: [("R2", j), ("L2", j)]}
        else:
            add(("R1", j), "xp", 2 * unit, [S, L], (j, 1))
            add(("L1", j), "xm", 2 * unit, [S, L], (j, 1))
            add(("R2", j), "xp", unit, [("R1", j)], (j, 0))
            add(("L2", j), "xm", unit, [("L1", j)], (j, 0))
            pre = {0: [S, L], -1: [("R1", j)], 1: [("L1", j)], 2: [("R2", j), ("L2", j)]}
            got = {}
            for d in (0, -1, 1, 2):
                add(("H", j, d), "zh", 2 * unit, pre[d], j)
                got[d] = pre[d] + [("H", j, d)]
        for d in (0, -1, 1, 2):
            add(("D", j, d), "dd", 4 * unit, got[d], j)
            need[j, d] = got[d] + [("D", j, d)]
        add(("Y", j), "zl", unit, [("C", j)], j)
    a_need = [("AS",)]
    for q in range(A_PIECES):
        add(("AL", q), "zl", a_unit, [("AS",)], 0.75 * q)
        for t in (0, 1):
            dep = [("AS",)] if t == 0 else [("AL", q)]
            add(("AR1", t, q), "yp", a_unit, dep, 4 * t + q)
            add(("AL1", t, q), "ym", a_unit, dep, 4 * t + q)
            a_need += [("AR1", t, q), ("AL1", t, q)]
        add(("AR2", q), "yp", a_unit, [("AR1", 0, q)], 8 + q)
        add(("AL2", q), "ym", a_unit, [("AL1", 1, q)], 8 + q)
        a_need += [("AL", q), ("AR2", q), ("AL2", q)]

    tasks = []
    for j in range(chunks):
        if j < chunks - 1:
            tasks += [(j, (0, -1)), (j, (1, 2))]
        else:
            tasks += [(j, (0,)), (j, (-1,)), (j, (1,)), (j, (2,))]

    prog = []
    t = 0.0
    at = {("AS",): 3.0}
    for j in range(chunks):
        at[("S", j)] = 2.5 + 0.3 * j
    done = set()
    waiting = dict(sends)
    busy = {k: 0.0 for k in RATE}
    out = {k: [] for k in RATE}
    loads = computed = 0
    while True:
        for link in RATE:
            out[link] = [e for e in out[link] if e > t]
            while len(out[link]) < DEPTH_Q:
                ready = [n for n, s in waiting.items() if s[0] == link and s[2] <= done]
                if not ready:
                    break
                name = min(ready, key=lambda n: (waiting[n][3], str(n)))
                size = waiting.pop(name)[1]
                busy[link] = max(busy[link], t + 0.2) + size / RATE[link]
                out[link].append(busy[link])
                at[name] = busy[link] + LAT.get(link, 2.0)
                prog.append(("start", name))
        if loads < len(tasks) and loads - computed < SLOTS:
            j, ds = tasks[loads]
            if all(set(need[j, d]) <= done for d in ds):
                prog.append(("load", loads))
                at["ld", loads] = t + 1.0 + 0.5 * len(ds)
                loads += 1
                continue
        now = sorted((v, str(n), n) for n, v in at.items() if n not in done and v <= t)
        if now:
            name = now[0][2]
            done.add(name)
            prog.append(("wait", name))
            continue
        if computed < loads and ("ld", computed) in done and set(a_need) <= done:
            prog.append(("compute", computed))
            j, ds = tasks[computed]
            t += 0.5 * half_us * len(ds)
            computed += 1
            if computed == len(tasks) or tasks[computed][0] != j:
                at["C", j] = t
                done.add(("C", j))
            continue
        later = [v for n, v in at.items() if n not in done]
        later += [e for link in RATE for e in out[link] if e > t]
        if not later:
            break
        t = min(later)
    if waiting or computed < len(tasks):
        raise ValueError("plan stuck")
    return prog, tasks, list(sends), t


def body(prog, tasks, names, modes, dims, a_ref, x_ref, y_ref, xg, av, xv, xs, yv, acc, ssem, rsem, lsem, osem, vsem):
    chunks, per_r, s, kb, width, kk = dims
    z, y, i = lax.axis_index("depth"), lax.axis_index("col"), lax.axis_index("row")
    x, c = i // 2, i % 2
    zh, pi = z // 2, z % 2
    nu = (zh + pi) % 2
    zl_peer = 2 * zh + 1 - pi
    zh_peer = 3 - z
    half = per_r * width

    def xat(d):
        return (x + d + 4) % 4

    def yat(d):
        return (y + d + 4) % 4

    dev = {
        "xp": (z, y, 2 * xat(1) + c),
        "xm": (z, y, 2 * xat(-1) + c),
        "yp": (z, yat(1), i),
        "ym": (z, yat(-1), i),
        "zl": (zl_peer, y, i),
        "zh": (zh_peer, y, i),
        "dd": (z, y, 2 * x + 1 - c),
    }

    def cols(j, part):
        return pl.ds(pl.multiple_of(part * half + (j % per_r) * width, 128), width)

    rows_a = s // A_PIECES

    def arow(which, q):
        return pl.ds(pl.multiple_of(which * s + q * rows_a, 16), rows_a)

    def krow(core, first, count):
        return pl.ds(pl.multiple_of((4 * core + first) * s, 16), count * s)

    def yrow(which):
        return pl.ds(pl.multiple_of(which * s, 16), s)

    def ends(name, recv):
        kind = name[0]
        if kind in ("AL", "AR1", "AL1", "AR2", "AL2"):
            q = name[-1]
            if kind == "AL":
                who = 1 - pi if recv else pi
                ref = av.at[y, arow(who, q)]
                return ref, ref, "zl"
            right = kind in ("AR1", "AR2")
            step = (-1 if right else 1) if recv else 0
            if kind in ("AR1", "AL1"):
                who = pi if name[1] == 0 else 1 - pi
                ref = av.at[yat(step), arow(who, q)]
            else:
                who = pi if right else 1 - pi
                ref = av.at[yat(step + (-1 if right else 1)), arow(who, q)]
            return ref, ref, "yp" if right else "ym"
        j = name[1]
        r = j // per_r
        if kind == "L":
            ref = xg.at[j, x, krow(c, zl_peer if recv else z, 1)]
            return (ref if recv else x_ref.at[r, :, cols(j, 1 - nu)]), ref, "zl"
        if kind == "Y":
            part = 1 - nu if recv else nu
            ref = y_ref.at[r, :, cols(j, part)]
            return yv.at[j, yrow(1 - pi)], ref, "zl"
        if kind == "D":
            ref = xg.at[j, xat(name[2]), krow(1 - c if recv else c, 0, 4)]
            return ref, ref, "dd"
        mine = krow(c, 2 * zh, 2)
        if kind == "H":
            d = name[2] if len(name) > 2 else 0
            ref = xg.at[j, xat(d), krow(c, 2 * (1 - zh), 2) if recv else mine]
            return ref, ref, "zh"
        right = kind[0] == "R"
        step = (-1 if right else 1) if recv else 0
        if modes[j] == "b":
            first = krow(c, 0, 4)
            second = krow(c, 0 if right else 2, 2)
        else:
            first = mine
            second = krow(c, 2 * zh if right else 2 * zh + 1, 1)
        if kind[1] == "1":
            ref = xg.at[j, xat(step), first]
        else:
            ref = xg.at[j, xat(step + (-1 if right else 1)), second]
        return ref, ref, "xp" if right else "xm"

    index = {n: k for k, n in enumerate(names)}

    def remote(name, recv=False):
        src, dst, link = ends(name, recv)
        return pltpu.make_async_remote_copy(
            src_ref=src, dst_ref=dst, send_sem=ssem.at[index[name]], recv_sem=rsem.at[index[name]],
            device_id=dev[link], device_id_type=MESH)

    def stage_in(j):
        return pltpu.make_async_copy(x_ref.at[j // per_r, :, cols(j, nu)], xs.at[j], lsem.at[j])

    def stage_out(j):
        return pltpu.make_async_copy(xs.at[j], xg.at[j, x, krow(c, z, 1)], lsem.at[chunks + j])

    def a_in():
        return pltpu.make_async_copy(a_ref, av.at[y, yrow(pi)], lsem.at[2 * chunks])

    def y_out(j):
        return pltpu.make_async_copy(yv.at[j, yrow(pi)], y_ref.at[j // per_r, :, cols(j, nu)], osem.at[j])

    def load(task, b):
        j, ds = tasks[task]
        slot = task % SLOTS
        return pltpu.make_async_copy(xg.at[j, xat(ds[b])], xv.at[slot, b], vsem.at[2 * slot + b])

    barrier = pltpu.get_barrier_semaphore()
    for peer in dev.values():
        pl.semaphore_signal(barrier, inc=1, device_id=peer, device_id_type=MESH)
    for j in range(chunks):
        stage_in(j).start()
    a_in().start()
    pl.semaphore_wait(barrier, len(dev))

    staged = [False]

    def finish_stage():
        for j in range(chunks):
            stage_in(j).wait()
            stage_out(j).start()
        staged[0] = True

    received = set()
    for op, what in prog:
        if op == "start":
            remote(what).start()
        elif op == "load":
            for b in range(len(tasks[what][1])):
                load(what, b).start()
        elif op == "wait":
            if not staged[0]:
                finish_stage()
            if what[0] == "S":
                stage_out(what[1]).wait()
            elif what[0] == "AS":
                a_in().wait()
            elif what[0] == "ld":
                for b in range(len(tasks[what[1]][1])):
                    load(what[1], b).wait()
            elif what[0] != "C":
                remote(what, True).wait_recv()
                received.add(what)
        else:
            j, ds = tasks[what]
            slot = what % SLOTS
            if what == 0 or tasks[what - 1][0] != j:
                acc[...] = jnp.zeros_like(acc)
            per = kb // kk
            base = ds[0]
            stride = ds[1] - ds[0] if len(ds) > 1 else 0

            def step(n, carry, slot=slot, base=base, stride=stride):
                b, k = n // per, n % per
                block = (x + base + 4 + stride * b) % 4
                lanes = pl.ds(pl.multiple_of(k * kk, 128), kk)
                acc[...] += jnp.dot(av[block, :, lanes], xv[slot, b, lanes, :], preferred_element_type=jnp.float32)
                return carry

            lax.fori_loop(0, per * len(ds), step, 0)
            if what + 1 == len(tasks) or tasks[what + 1][0] != j:
                yv[j] = acc[...].astype(yv.dtype)
                y_out(j).start()

    for name in names:
        if name not in received:
            remote(name, True).wait_recv()
    for name in names:
        remote(name).wait_send()
    for j in range(chunks):
        y_out(j).wait()


def solution(mesh):
    def local(a, x):
        rhs, s, xc = x.shape
        kb = a.shape[1]
        width = 256 if xc % 512 == 0 else xc // 2
        per_r = xc // 2 // width
        chunks = rhs * per_r
        modes = (MODES * chunks)[:chunks]
        kk = 1024 if kb % 1024 == 0 else 256
        prog, tasks, names, _ = make_plan(chunks, modes, 2 * s * width, 2 * s * kb // A_PIECES, 2.9)
        dims = (chunks, per_r, s, kb, width, kk)
        any_spec = pl.BlockSpec(memory_space=pl.ANY)
        y, _ = pl.pallas_call(
            functools.partial(body, prog, tasks, names, modes, dims),
            out_shape=(jax.ShapeDtypeStruct(x.shape, x.dtype), jax.ShapeDtypeStruct((chunks, 4, kb, width), x.dtype)),
            in_specs=[any_spec, any_spec],
            out_specs=(any_spec, any_spec),
            scratch_shapes=[
                pltpu.VMEM((4, 2 * s, kb), a.dtype),
                pltpu.VMEM((SLOTS, 2, kb, width), x.dtype),
                pltpu.VMEM((chunks, s, width), x.dtype),
                pltpu.VMEM((chunks, 2 * s, width), x.dtype),
                pltpu.VMEM((2 * s, width), jnp.float32),
                pltpu.SemaphoreType.DMA((len(names),)),
                pltpu.SemaphoreType.DMA((len(names),)),
                pltpu.SemaphoreType.DMA((2 * chunks + 1,)),
                pltpu.SemaphoreType.DMA((chunks,)),
                pltpu.SemaphoreType.DMA((2 * SLOTS,)),
            ],
            compiler_params=pltpu.CompilerParams(collective_id=0, has_side_effects=True, vmem_limit_bytes=60 * 1024 * 1024),
        )(a, x)
        return y

    spec_a = P(("row", "depth"), "col")
    spec_x = P(None, ("row", "depth"), "col")
    return jax.shard_map(local, mesh=mesh, in_specs=(spec_a, spec_x), out_specs=spec_x, check_vma=False)
```

time: 1620 us -> 294 us (0.18)
  waiting for transfers between devices: 1130 us -> 0 us
  Pallas kernels: 0 us -> 288 us
  starting transfers between devices: 286 us -> 0 us
  matrix products: 78.8 us -> 0 us
  local copies, waits for them, and re-layouts: 64.1 us -> 5.24 us
  other arithmetic: 36.8 us -> 0 us
    reduce_scatter x1 -> x0, waiting for transfers between devices: 524 us -> none  [local_product(): lax.psum_scatter(partial_sum, 'depth', scatter_dimension=1, tiled=True)]
    ppermute x6 -> x0, waiting for transfers between devices: 433 us -> none  [the longest x1 230 us: local_product(): w_next = lax.ppermute(w_layer, ALL_AXES, perm_a_next)]
    pallas_call x0 -> x1, Pallas kernels: none -> 288 us  [local(): pl.pallas_call(functools.partial(body, prog, tasks, names, modes, dims),...]
    ppermute x6 -> x0, starting transfers between devices: 285 us -> none  [the longest x1 205 us: local_product(): w_next = lax.ppermute(w_layer, ALL_AXES, perm_a_next)]
    all_gather x2 -> x0, waiting for transfers between devices: 173 us -> none  [the longest x1 173 us: local_product(): x_layer = lax.all_gather(x_split, 'depth', axis=1, tiled=True)]
    dot_general x2 -> x0, matrix products: 78.8 us -> none  [local_product(): jnp.einsum('tik,tkrm->tirm', w_blocks, x_blocks, preferred_element_type=j...]
    concatenate x1 -> x0, other arithmetic: 20.6 us -> none  [local_product(): jnp.concatenate([w_near, w_next], axis=1)]
    unnamed x9 -> x1, local copies, waits for them, and re-layouts: 21.7 us -> 5.24 us
  transfers between devices with their start and end apart: 9 -> 0, of which waited for: 5 -> 0; matrix products, arithmetic and copies ran while one was open for 4% -> 0% of each run, Pallas kernels for 0% -> 0%
where the time goes in v1:
time: 294 us; the launch traced here: 293 us
  Pallas kernels  288 us (98%)
  local copies, waits for them, and re-layouts  5.24 us (2%)
    pallas_call x1, Pallas kernels, local(): pl.pallas_call(functools.partial(body, prog, tasks, names, modes, dims),...  288 us

profile of v1, /device:TPU:0, one launch (start us, length us, event | category | flops | bytes accessed | tf_op | source)
XLA Modules:
  0.0 293.4 jit_solution(11311896683572890099)
XLA Ops:
  0.0 288.2 %shard_map.28 = (bf16[3,384,2048]{2,1,0:T(8,128)(2,1)}, bf16[12,4,3072,256]{3,2,1,0:T(8,128)(2,1)}) custom-call(bf16[384,3072]{1,0:T(8,128)(2,1)} %a_ref.1, bf16[3,384,2048]{2,1,0:T(8,128)(2,1)} %x_ref.1), custom_call_target="tpu_custom_call" | custom-call | tf_op jit(solution)/shard_map/pallas_call | solution.py:315
  288.2 5.2 %copy.4 = bf16[3,384,2048]{2,1,0:T(8,128)(2,1)} copy(bf16[3,384,2048]{2,1,0:T(8,128)(2,1)} %get-tuple-element.6) | data formatting | bytes 9437184

commit v2 on v1

--- a/solution.py
+++ b/solution.py
@@ -8,7 +8,7 @@
 from jax.sharding import PartitionSpec as P
 
 MESH = pl.DeviceIdType.MESH
-MODES = "babababbabab"
+MODES = "abbabbaabbabb"
 A_PIECES = 4
 SLOTS = 3
 DEPTH_Q = 2
@@ -16,29 +16,34 @@
 LAT = {"dd": 1.5}
 
 
-def make_plan(chunks, modes, unit, a_unit, half_us):
+def make_plan(units, modes, a_unit, half_us):
     sends = {}
+    chunks = len(units)
 
     def add(name, link, size, deps, key):
         sends[name] = (link, size, frozenset(deps), key)
 
     need = {}
     for j in range(chunks):
-        S, L = ("S", j), ("L", j)
+        S, L, unit = ("S", j), ("L", j), units[j]
         add(L, "zl", unit, [], j - 1)
         if modes[j] == "b":
-            add(("H", j), "zh", 2 * unit, [S, L], j - 1.5)
-            add(("R1", j), "xp", 4 * unit, [S, L, ("H", j)], (j, 1))
-            add(("L1", j), "xm", 4 * unit, [S, L, ("H", j)], (j, 1))
-            add(("R2", j), "xp", 2 * unit, [("R1", j)], (j, 0))
-            add(("L2", j), "xm", 2 * unit, [("L1", j)], (j, 0))
-            got = {0: [S, L, ("H", j)], -1: [("R1", j)], 1: [("L1", j)], 2: [("R2", j), ("L2", j)]}
+            add(("H", j, 0), "zh", unit, [], j - 1.5)
+            add(("H", j, 1), "zh", unit, [L], j - 1.5)
+            h = [("H", j, 0), ("H", j, 1)]
+            for way, link in (("R", "xp"), ("L", "xm")):
+                add((way + "1", j, 0), link, 2 * unit, [S, L], (j, 1))
+                add((way + "1", j, 1), link, 2 * unit, h, (j, 1))
+            add(("R2", j), "xp", 2 * unit, [("R1", j, 0)], (j, 0))
+            add(("L2", j), "xm", 2 * unit, [("L1", j, 1)], (j, 0))
+            got = {0: [S, L] + h, -1: [("R1", j, 0), ("R1", j, 1)], 1: [("L1", j, 0), ("L1", j, 1)], 2: [("R2", j), ("L2", j)]}
         else:
-            add(("R1", j), "xp", 2 * unit, [S, L], (j, 1))
-            add(("L1", j), "xm", 2 * unit, [S, L], (j, 1))
-            add(("R2", j), "xp", unit, [("R1", j)], (j, 0))
-            add(("L2", j), "xm", unit, [("L1", j)], (j, 0))
-            pre = {0: [S, L], -1: [("R1", j)], 1: [("L1", j)], 2: [("R2", j), ("L2", j)]}
+            for way, link in (("R", "xp"), ("L", "xm")):
+                add((way + "1", j, 0), link, unit, [], (j, 1))
+                add((way + "1", j, 1), link, unit, [L], (j, 1))
+            add(("R2", j), "xp", unit, [("R1", j, 0)], (j, 0))
+            add(("L2", j), "xm", unit, [("L1", j, 1)], (j, 0))
+            pre = {0: [S, L], -1: [("R1", j, 0), ("R1", j, 1)], 1: [("L1", j, 0), ("L1", j, 1)], 2: [("R2", j), ("L2", j)]}
             got = {}
             for d in (0, -1, 1, 2):
                 add(("H", j, d), "zh", 2 * unit, pre[d], j)
@@ -122,14 +127,14 @@
 
 
 def body(prog, tasks, names, modes, dims, a_ref, x_ref, y_ref, xg, av, xv, xs, yv, acc, ssem, rsem, lsem, osem, vsem):
-    chunks, per_r, s, kb, width, kk = dims
+    layout, s, kb, half, kk = dims
+    chunks = len(layout)
     z, y, i = lax.axis_index("depth"), lax.axis_index("col"), lax.axis_index("row")
     x, c = i // 2, i % 2
     zh, pi = z // 2, z % 2
     nu = (zh + pi) % 2
     zl_peer = 2 * zh + 1 - pi
     zh_peer = 3 - z
-    half = per_r * width
 
     def xat(d):
         return (x + d + 4) % 4
@@ -148,7 +153,16 @@
     }
 
     def cols(j, part):
-        return pl.ds(pl.multiple_of(part * half + (j % per_r) * width, 128), width)
+        return pl.ds(pl.multiple_of(part * half + layout[j][1], 128), layout[j][2])
+
+    def lane(j):
+        return pl.ds(0, layout[j][2])
+
+    def xin(j, part):
+        return x_ref.at[layout[j][0], :, cols(j, part)]
+
+    def xgat(j, block, rows):
+        return xg.at[j, block, rows, lane(j)]
 
     rows_a = s // A_PIECES
 
@@ -179,35 +193,37 @@
                 ref = av.at[yat(step + (-1 if right else 1)), arow(who, q)]
             return ref, ref, "yp" if right else "ym"
         j = name[1]
-        r = j // per_r
         if kind == "L":
-            ref = xg.at[j, x, krow(c, zl_peer if recv else z, 1)]
-            return (ref if recv else x_ref.at[r, :, cols(j, 1 - nu)]), ref, "zl"
+            ref = xgat(j, x, krow(c, zl_peer if recv else z, 1))
+            return (ref if recv else xin(j, 1 - nu)), ref, "zl"
         if kind == "Y":
             part = 1 - nu if recv else nu
-            ref = y_ref.at[r, :, cols(j, part)]
-            return yv.at[j, yrow(1 - pi)], ref, "zl"
+            ref = y_ref.at[layout[j][0], :, cols(j, part)]
+            return yv.at[j, yrow(1 - pi), lane(j)], ref, "zl"
         if kind == "D":
-            ref = xg.at[j, xat(name[2]), krow(1 - c if recv else c, 0, 4)]
+            ref = xgat(j, xat(name[2]), krow(1 - c if recv else c, 0, 4))
             return ref, ref, "dd"
-        mine = krow(c, 2 * zh, 2)
+        own, pair, other = krow(c, z, 1), krow(c, 2 * zh, 2), krow(c, 2 * (1 - zh), 2)
         if kind == "H":
-            d = name[2] if len(name) > 2 else 0
-            ref = xg.at[j, xat(d), krow(c, 2 * (1 - zh), 2) if recv else mine]
+            if modes[j] == "b":
+                at = z if name[2] == 0 else zl_peer
+                ref = xgat(j, x, krow(c, 3 - at if recv else at, 1))
+                return (xin(j, nu) if name[2] == 0 and not recv else ref), ref, "zh"
+            ref = xgat(j, xat(name[2]), other if recv else pair)
             return ref, ref, "zh"
         right = kind[0] == "R"
+        link = "xp" if right else "xm"
         step = (-1 if right else 1) if recv else 0
         if modes[j] == "b":
-            first = krow(c, 0, 4)
-            second = krow(c, 0 if right else 2, 2)
+            parts = (pair, other)
         else:
-            first = mine
-            second = krow(c, 2 * zh if right else 2 * zh + 1, 1)
+            parts = (own, krow(c, zl_peer, 1))
         if kind[1] == "1":
-            ref = xg.at[j, xat(step), first]
-        else:
-            ref = xg.at[j, xat(step + (-1 if right else 1)), second]
-        return ref, ref, "xp" if right else "xm"
+            ref = xgat(j, xat(step), parts[name[2]])
+            direct = modes[j] == "a" and name[2] == 0 and not recv
+            return (xin(j, nu) if direct else ref), ref, link
+        ref = xgat(j, xat(step + (-1 if right else 1)), parts[0 if right else 1])
+        return ref, ref, link
 
     index = {n: k for k, n in enumerate(names)}
 
@@ -218,21 +234,21 @@
             device_id=dev[link], device_id_type=MESH)
 
     def stage_in(j):
-        return pltpu.make_async_copy(x_ref.at[j // per_r, :, cols(j, nu)], xs.at[j], lsem.at[j])
+        return pltpu.make_async_copy(xin(j, nu), xs.at[j, :, lane(j)], lsem.at[j])
 
     def stage_out(j):
-        return pltpu.make_async_copy(xs.at[j], xg.at[j, x, krow(c, z, 1)], lsem.at[chunks + j])
+        return pltpu.make_async_copy(xs.at[j, :, lane(j)], xgat(j, x, krow(c, z, 1)), lsem.at[chunks + j])
 
     def a_in():
         return pltpu.make_async_copy(a_ref, av.at[y, yrow(pi)], lsem.at[2 * chunks])
 
     def y_out(j):
-        return pltpu.make_async_copy(yv.at[j, yrow(pi)], y_ref.at[j // per_r, :, cols(j, nu)], osem.at[j])
+        return pltpu.make_async_copy(yv.at[j, yrow(pi), lane(j)], y_ref.at[layout[j][0], :, cols(j, nu)], osem.at[j])
 
     def load(task, b):
         j, ds = tasks[task]
         slot = task % SLOTS
-        return pltpu.make_async_copy(xg.at[j, xat(ds[b])], xv.at[slot, b], vsem.at[2 * slot + b])
+        return pltpu.make_async_copy(xgat(j, xat(ds[b]), pl.ds(0, kb)), xv.at[slot, b, :, lane(j)], vsem.at[2 * slot + b])
 
     barrier = pltpu.get_barrier_semaphore()
     for peer in dev.values():
@@ -274,21 +290,21 @@
             j, ds = tasks[what]
             slot = what % SLOTS
             if what == 0 or tasks[what - 1][0] != j:
-                acc[...] = jnp.zeros_like(acc)
+                acc[:, lane(j)] = jnp.zeros((2 * s, layout[j][2]), jnp.float32)
             per = kb // kk
             base = ds[0]
             stride = ds[1] - ds[0] if len(ds) > 1 else 0
 
-            def step(n, carry, slot=slot, base=base, stride=stride):
+            def step(n, carry, slot=slot, base=base, stride=stride, wide=lane(j)):
                 b, k = n // per, n % per
                 block = (x + base + 4 + stride * b) % 4
                 lanes = pl.ds(pl.multiple_of(k * kk, 128), kk)
-                acc[...] += jnp.dot(av[block, :, lanes], xv[slot, b, lanes, :], preferred_element_type=jnp.float32)
+                acc[:, wide] += jnp.dot(av[block, :, lanes], xv[slot, b, lanes, wide], preferred_element_type=jnp.float32)
                 return carry
 
             lax.fori_loop(0, per * len(ds), step, 0)
             if what + 1 == len(tasks) or tasks[what + 1][0] != j:
-                yv[j] = acc[...].astype(yv.dtype)
+                yv[j, :, lane(j)] = acc[:, lane(j)].astype(yv.dtype)
                 y_out(j).start()
 
     for name in names:
@@ -304,13 +320,18 @@
     def local(a, x):
         rhs, s, xc = x.shape
         kb = a.shape[1]
-        width = 256 if xc % 512 == 0 else xc // 2
-        per_r = xc // 2 // width
-        chunks = rhs * per_r
+        half = xc // 2
+        width = 256 if half % 256 == 0 else 128
+        layout = [(r, at, width) for r in range(rhs) for at in range(0, half, width)]
+        if width == 256:
+            r, at, _ = layout.pop()
+            layout += [(r, at, 128), (r, at + 128, 128)]
+        chunks = len(layout)
         modes = (MODES * chunks)[:chunks]
         kk = 1024 if kb % 1024 == 0 else 256
-        prog, tasks, names, _ = make_plan(chunks, modes, 2 * s * width, 2 * s * kb // A_PIECES, 2.9)
-        dims = (chunks, per_r, s, kb, width, kk)
+        units = [2 * s * w for _, _, w in layout]
+        prog, tasks, names, _ = make_plan(units, modes, 2 * s * kb // A_PIECES, 2.9)
+        dims = (layout, s, kb, half, kk)
         any_spec = pl.BlockSpec(memory_space=pl.ANY)
         y, _ = pl.pallas_call(
             functools.partial(body, prog, tasks, names, modes, dims),

time: 294 us -> 289 us (0.983)
  Pallas kernels: 288 us -> 282 us
    pallas_call x1, Pallas kernels: 288 us -> 282 us  [local(): pl.pallas_call(functools.partial(body, prog, tasks, names, modes, dims),...]
where the time goes in v2:
time: 289 us; the launch traced here: 287 us
  Pallas kernels  282 us (98%)
  local copies, waits for them, and re-layouts  5.24 us (2%)
    pallas_call x1, Pallas kernels, local(): pl.pallas_call(functools.partial(body, prog, tasks, names, modes, dims),...  282 us

profile of v2, /device:TPU:0, one launch (start us, length us, event | category | flops | bytes accessed | tf_op | source)
XLA Modules:
  0.0 287.2 jit_solution(3993643699449067691)
XLA Ops:
  0.0 282.0 %shard_map.28 = (bf16[3,384,2048]{2,1,0:T(8,128)(2,1)}, bf16[13,4,3072,256]{3,2,1,0:T(8,128)(2,1)}) custom-call(bf16[384,3072]{1,0:T(8,128)(2,1)} %a_ref.1, bf16[3,384,2048]{2,1,0:T(8,128)(2,1)} %x_ref.1), custom_call_target="tpu_custom_call" | custom-call | tf_op jit(solution)/shard_map/pallas_call | solution.py:336
  282.0 5.2 %copy.4 = bf16[3,384,2048]{2,1,0:T(8,128)(2,1)} copy(bf16[3,384,2048]{2,1,0:T(8,128)(2,1)} %get-tuple-element.6) | data formatting | bytes 9437184

commit v3 on v2

--- a/solution.py
+++ b/solution.py
@@ -10,13 +10,17 @@
 MESH = pl.DeviceIdType.MESH
 MODES = "abbabbaabbabb"
 A_PIECES = 4
-SLOTS = 3
-DEPTH_Q = 2
-RATE = {"xp": 46.0e3, "xm": 46.0e3, "yp": 46.0e3, "ym": 46.0e3, "zl": 46.0e3, "zh": 46.0e3, "dd": 250.0e3}
-LAT = {"dd": 1.5}
-
-
-def make_plan(units, modes, a_unit, half_us):
+SLOTS = 5
+DEPTH_Q = 3
+TAIL_CHUNKS = 2
+MARGIN = 2.0
+PLAN_LAT = 2.5
+BLOCK_US = 1.8
+RATE = {"xp": 46.0e3, "xm": 46.0e3, "yp": 46.0e3, "ym": 46.0e3, "zl": 46.0e3, "zh": 46.0e3, "dd": 200.0e3}
+LAT = {"dd": 2.5}
+
+
+def make_plan(units, modes, a_unit, block_us):
     sends = {}
     chunks = len(units)
 
@@ -52,76 +56,100 @@
             add(("D", j, d), "dd", 4 * unit, got[d], j)
             need[j, d] = got[d] + [("D", j, d)]
         add(("Y", j), "zl", unit, [("C", j)], j)
-    a_need = [("AS",)]
+    a_need = {0: [("AS",)], 1: [], -1: [], 2: []}
     for q in range(A_PIECES):
         add(("AL", q), "zl", a_unit, [("AS",)], 0.75 * q)
         for t in (0, 1):
             dep = [("AS",)] if t == 0 else [("AL", q)]
             add(("AR1", t, q), "yp", a_unit, dep, 4 * t + q)
             add(("AL1", t, q), "ym", a_unit, dep, 4 * t + q)
-            a_need += [("AR1", t, q), ("AL1", t, q)]
+            a_need[-1].append(("AR1", t, q))
+            a_need[1].append(("AL1", t, q))
         add(("AR2", q), "yp", a_unit, [("AR1", 0, q)], 8 + q)
         add(("AL2", q), "ym", a_unit, [("AL1", 1, q)], 8 + q)
-        a_need += [("AL", q), ("AR2", q), ("AL2", q)]
+        a_need[0].append(("AL", q))
+        a_need[2] += [("AR2", q), ("AL2", q)]
+    a_all = sum(a_need.values(), [])
 
     tasks = []
-    for j in range(chunks):
-        if j < chunks - 1:
-            tasks += [(j, (0, -1)), (j, (1, 2))]
-        else:
-            tasks += [(j, (0,)), (j, (-1,)), (j, (1,)), (j, (2,))]
+    left = []
+    for j in range(chunks):
+        for e in (0, -1, 1, 2):
+            if j < chunks - TAIL_CHUNKS:
+                left.append((j, "y", e, sum((need[j, d] for d in (0, -1, 1, 2)), []), a_need[e]))
+            else:
+                left.append((j, "x", e, need[j, e], a_all))
 
     prog = []
     t = 0.0
     at = {("AS",): 3.0}
     for j in range(chunks):
         at[("S", j)] = 2.5 + 0.3 * j
+    eager = set().union(*(v[2] for v in sends.values()))
     done = set()
     waiting = dict(sends)
     busy = {k: 0.0 for k in RATE}
     out = {k: [] for k in RATE}
-    loads = computed = 0
+    ready_at = {}
+    computed = 0
+    parts = {}
+
+    def arrived(events, when):
+        return all(n in done or at.get(n, 1e9) <= when for n in events)
+
+    def settle(events):
+        for n in events:
+            if n not in done:
+                done.add(n)
+                prog.append(("wait", n))
+
     while True:
         for link in RATE:
             out[link] = [e for e in out[link] if e > t]
             while len(out[link]) < DEPTH_Q:
-                ready = [n for n, s in waiting.items() if s[0] == link and s[2] <= done]
+                ready = [n for n, v in waiting.items() if v[0] == link and v[2] <= done]
                 if not ready:
                     break
                 name = min(ready, key=lambda n: (waiting[n][3], str(n)))
                 size = waiting.pop(name)[1]
                 busy[link] = max(busy[link], t + 0.2) + size / RATE[link]
                 out[link].append(busy[link])
-                at[name] = busy[link] + LAT.get(link, 2.0)
+                at[name] = busy[link] + LAT.get(link, PLAN_LAT)
                 prog.append(("start", name))
-        if loads < len(tasks) and loads - computed < SLOTS:
-            j, ds = tasks[loads]
-            if all(set(need[j, d]) <= done for d in ds):
-                prog.append(("load", loads))
-                at["ld", loads] = t + 1.0 + 0.5 * len(ds)
-                loads += 1
+        now = sorted((v, str(n), n) for n, v in at.items() if n in eager and n not in done and v <= t)
+        if now:
+            settle([now[0][2]])
+            continue
+        margin = MARGIN if len(left) > 4 * TAIL_CHUNKS else 0.0
+        if len(tasks) - computed < SLOTS:
+            pick = [v for v in left if arrived(v[3], t - margin) and arrived(v[4], t - margin)]
+            if pick:
+                task = pick[0]
+                left.remove(task)
+                settle(task[3])
+                settle(task[4])
+                prog.append(("load", len(tasks)))
+                ready_at[len(tasks)] = t + 1.7
+                tasks.append(task[:3])
                 continue
-        now = sorted((v, str(n), n) for n, v in at.items() if n not in done and v <= t)
-        if now:
-            name = now[0][2]
-            done.add(name)
-            prog.append(("wait", name))
-            continue
-        if computed < loads and ("ld", computed) in done and set(a_need) <= done:
+        if computed < len(tasks) and ready_at[computed] <= t:
             prog.append(("compute", computed))
-            j, ds = tasks[computed]
-            t += 0.5 * half_us * len(ds)
+            j = tasks[computed][0]
+            t += block_us
             computed += 1
-            if computed == len(tasks) or tasks[computed][0] != j:
-                at["C", j] = t
+            parts[j] = parts.get(j, 0) + 1
+            if parts[j] == 4:
                 done.add(("C", j))
             continue
-        later = [v for n, v in at.items() if n not in done]
+        later = [v for n, v in at.items() if n in eager and n not in done]
         later += [e for link in RATE for e in out[link] if e > t]
+        later += [v for k, v in ready_at.items() if k >= computed]
+        later += [v + margin for n, v in at.items() if n not in done and v + margin > t]
+        later = [v for v in later if v > t]
         if not later:
             break
         t = min(later)
-    if waiting or computed < len(tasks):
+    if waiting or left or computed < len(tasks):
         raise ValueError("plan stuck")
     return prog, tasks, list(sends), t
 
@@ -245,10 +273,11 @@
     def y_out(j):
         return pltpu.make_async_copy(yv.at[j, yrow(pi), lane(j)], y_ref.at[layout[j][0], :, cols(j, nu)], osem.at[j])
 
-    def load(task, b):
-        j, ds = tasks[task]
+    def load(task):
+        j, axis, e = tasks[task]
         slot = task % SLOTS
-        return pltpu.make_async_copy(xgat(j, xat(ds[b]), pl.ds(0, kb)), xv.at[slot, b, :, lane(j)], vsem.at[2 * slot + b])
+        block = yat(e) if axis == "y" else xat(e)
+        return pltpu.make_async_copy(xgat(j, block, pl.ds(0, kb)), xv.at[slot, :, lane(j)], vsem.at[slot])
 
     barrier = pltpu.get_barrier_semaphore()
     for peer in dev.values():
@@ -267,12 +296,12 @@
         staged[0] = True
 
     received = set()
+    parts = [0] * chunks
     for op, what in prog:
         if op == "start":
             remote(what).start()
         elif op == "load":
-            for b in range(len(tasks[what][1])):
-                load(what, b).start()
+            load(what).start()
         elif op == "wait":
             if not staged[0]:
                 finish_stage()
@@ -280,31 +309,27 @@
                 stage_out(what[1]).wait()
             elif what[0] == "AS":
                 a_in().wait()
-            elif what[0] == "ld":
-                for b in range(len(tasks[what[1]][1])):
-                    load(what[1], b).wait()
-            elif what[0] != "C":
+            else:
                 remote(what, True).wait_recv()
                 received.add(what)
         else:
-            j, ds = tasks[what]
+            j, axis, e = tasks[what]
             slot = what % SLOTS
-            if what == 0 or tasks[what - 1][0] != j:
-                acc[:, lane(j)] = jnp.zeros((2 * s, layout[j][2]), jnp.float32)
-            per = kb // kk
-            base = ds[0]
-            stride = ds[1] - ds[0] if len(ds) > 1 else 0
-
-            def step(n, carry, slot=slot, base=base, stride=stride, wide=lane(j)):
-                b, k = n // per, n % per
-                block = (x + base + 4 + stride * b) % 4
+            wide = lane(j)
+            load(what).wait()
+            if parts[j] == 0:
+                acc[j, :, wide] = jnp.zeros((2 * s, layout[j][2]), jnp.float32)
+            block = yat(e) if axis == "y" else xat(e)
+
+            def step(k, carry, slot=slot, block=block, j=j, wide=wide):
                 lanes = pl.ds(pl.multiple_of(k * kk, 128), kk)
-                acc[:, wide] += jnp.dot(av[block, :, lanes], xv[slot, b, lanes, wide], preferred_element_type=jnp.float32)
+                acc[j, :, wide] += jnp.dot(av[block, :, lanes], xv[slot, lanes, wide], preferred_element_type=jnp.float32)
                 return carry
 
-            lax.fori_loop(0, per * len(ds), step, 0)
-            if what + 1 == len(tasks) or tasks[what + 1][0] != j:
-                yv[j, :, lane(j)] = acc[:, lane(j)].astype(yv.dtype)
+            lax.fori_loop(0, kb // kk, step, 0)
+            parts[j] += 1
+            if parts[j] == 4:
+                yv[j, :, wide] = acc[j, :, wide].astype(yv.dtype)
                 y_out(j).start()
 
     for name in names:
@@ -330,7 +355,7 @@
         modes = (MODES * chunks)[:chunks]
         kk = 1024 if kb % 1024 == 0 else 256
         units = [2 * s * w for _, _, w in layout]
-        prog, tasks, names, _ = make_plan(units, modes, 2 * s * kb // A_PIECES, 2.9)
+        prog, tasks, names, _ = make_plan(units, modes, 2 * s * kb // A_PIECES, BLOCK_US)
         dims = (layout, s, kb, half, kk)
         any_spec = pl.BlockSpec(memory_space=pl.ANY)
         y, _ = pl.pallas_call(
@@ -340,15 +365,15 @@
             out_specs=(any_spec, any_spec),
             scratch_shapes=[
                 pltpu.VMEM((4, 2 * s, kb), a.dtype),
-                pltpu.VMEM((SLOTS, 2, kb, width), x.dtype),
+                pltpu.VMEM((SLOTS, kb, width), x.dtype),
                 pltpu.VMEM((chunks, s, width), x.dtype),
                 pltpu.VMEM((chunks, 2 * s, width), x.dtype),
-                pltpu.VMEM((2 * s, width), jnp.float32),
+                pltpu.VMEM((chunks, 2 * s, width), jnp.float32),
                 pltpu.SemaphoreType.DMA((len(names),)),
                 pltpu.SemaphoreType.DMA((len(names),)),
                 pltpu.SemaphoreType.DMA((2 * chunks + 1,)),
                 pltpu.SemaphoreType.DMA((chunks,)),
-                pltpu.SemaphoreType.DMA((2 * SLOTS,)),
+                pltpu.SemaphoreType.DMA((SLOTS,)),
             ],
             compiler_params=pltpu.CompilerParams(collective_id=0, has_side_effects=True, vmem_limit_bytes=60 * 1024 * 1024),
         )(a, x)

time: 289 us -> 275 us (0.952)
  Pallas kernels: 282 us -> 270 us
    pallas_call x1, Pallas kernels: 282 us -> 270 us  [local(): pl.pallas_call(functools.partial(body, prog, tasks, names, modes, dims),...]
where the time goes in v3:
time: 275 us
  Pallas kernels  270 us (98%)
  local copies, waits for them, and re-layouts  5.24 us (2%)
    pallas_call x1, Pallas kernels, local(): pl.pallas_call(functools.partial(body, prog, tasks, names, modes, dims),...  270 us

profile of v3, /device:TPU:0, one launch (start us, length us, event | category | flops | bytes accessed | tf_op | source)
XLA Modules:
  0.0 275.1 jit_solution(18320716872995496476)
XLA Ops:
  0.0 269.9 %shard_map.28 = (bf16[3,384,2048]{2,1,0:T(8,128)(2,1)}, bf16[13,4,3072,256]{3,2,1,0:T(8,128)(2,1)}) custom-call(bf16[384,3072]{1,0:T(8,128)(2,1)} %a_ref.1, bf16[3,384,2048]{2,1,0:T(8,128)(2,1)} %x_ref.1), custom_call_target="tpu_custom_call" | custom-call | tf_op jit(solution)/shard_map/pallas_call | solution.py:361
  269.9 5.2 %copy.4 = bf16[3,384,2048]{2,1,0:T(8,128)(2,1)} copy(bf16[3,384,2048]{2,1,0:T(8,128)(2,1)} %get-tuple-element.6) | data formatting | bytes 9437184

commit v4 on v3

--- a/solution.py
+++ b/solution.py
@@ -129,7 +129,7 @@
                 settle(task[3])
                 settle(task[4])
                 prog.append(("load", len(tasks)))
-                ready_at[len(tasks)] = t + 1.7
+                ready_at[len(tasks)] = t + 1.7 if task[0] < chunks - 1 else t
                 tasks.append(task[:3])
                 continue
         if computed < len(tasks) and ready_at[computed] <= t:
@@ -154,7 +154,7 @@
     return prog, tasks, list(sends), t
 
 
-def body(prog, tasks, names, modes, dims, a_ref, x_ref, y_ref, xg, av, xv, xs, yv, acc, ssem, rsem, lsem, osem, vsem):
+def body(prog, tasks, names, modes, dims, a_ref, x_ref, y_ref, xg, av, xv, xt, xs, yv, acc, ssem, rsem, lsem, vsem):
     layout, s, kb, half, kk = dims
     chunks = len(layout)
     z, y, i = lax.axis_index("depth"), lax.axis_index("col"), lax.axis_index("row")
@@ -190,6 +190,8 @@
         return x_ref.at[layout[j][0], :, cols(j, part)]
 
     def xgat(j, block, rows):
+        if j == chunks - 1:
+            return xt.at[block, rows]
         return xg.at[j, block, rows, lane(j)]
 
     rows_a = s // A_PIECES
@@ -227,7 +229,7 @@
         if kind == "Y":
             part = 1 - nu if recv else nu
             ref = y_ref.at[layout[j][0], :, cols(j, part)]
-            return yv.at[j, yrow(1 - pi), lane(j)], ref, "zl"
+            return yv.at[j, :, lane(j)], ref, "zl"
         if kind == "D":
             ref = xgat(j, xat(name[2]), krow(1 - c if recv else c, 0, 4))
             return ref, ref, "dd"
@@ -262,16 +264,14 @@
             device_id=dev[link], device_id_type=MESH)
 
     def stage_in(j):
-        return pltpu.make_async_copy(xin(j, nu), xs.at[j, :, lane(j)], lsem.at[j])
+        dst = xgat(j, x, krow(c, z, 1)) if j == chunks - 1 else xs.at[j, :, lane(j)]
+        return pltpu.make_async_copy(xin(j, nu), dst, lsem.at[j])
 
     def stage_out(j):
         return pltpu.make_async_copy(xs.at[j, :, lane(j)], xgat(j, x, krow(c, z, 1)), lsem.at[chunks + j])
 
     def a_in():
         return pltpu.make_async_copy(a_ref, av.at[y, yrow(pi)], lsem.at[2 * chunks])
-
-    def y_out(j):
-        return pltpu.make_async_copy(yv.at[j, yrow(pi), lane(j)], y_ref.at[layout[j][0], :, cols(j, nu)], osem.at[j])
 
     def load(task):
         j, axis, e = tasks[task]
@@ -290,7 +290,7 @@
     staged = [False]
 
     def finish_stage():
-        for j in range(chunks):
+        for j in range(chunks - 1):
             stage_in(j).wait()
             stage_out(j).start()
         staged[0] = True
@@ -301,12 +301,13 @@
         if op == "start":
             remote(what).start()
         elif op == "load":
-            load(what).start()
+            if tasks[what][0] < chunks - 1:
+                load(what).start()
         elif op == "wait":
             if not staged[0]:
                 finish_stage()
             if what[0] == "S":
-                stage_out(what[1]).wait()
+                (stage_in if what[1] == chunks - 1 else stage_out)(what[1]).wait()
             elif what[0] == "AS":
                 a_in().wait()
             else:
@@ -316,29 +317,31 @@
             j, axis, e = tasks[what]
             slot = what % SLOTS
             wide = lane(j)
-            load(what).wait()
+            if j < chunks - 1:
+                load(what).wait()
             if parts[j] == 0:
                 acc[j, :, wide] = jnp.zeros((2 * s, layout[j][2]), jnp.float32)
             block = yat(e) if axis == "y" else xat(e)
 
-            def step(k, carry, slot=slot, block=block, j=j, wide=wide):
+            def rhs(lanes, slot=slot, block=block, j=j, wide=wide):
+                return xt[block, lanes, :] if j == chunks - 1 else xv[slot, lanes, wide]
+
+            def step(k, carry, rhs=rhs, block=block, j=j, wide=wide):
                 lanes = pl.ds(pl.multiple_of(k * kk, 128), kk)
-                acc[j, :, wide] += jnp.dot(av[block, :, lanes], xv[slot, lanes, wide], preferred_element_type=jnp.float32)
+                acc[j, :, wide] += jnp.dot(av[block, :, lanes], rhs(lanes), preferred_element_type=jnp.float32)
                 return carry
 
             lax.fori_loop(0, kb // kk, step, 0)
             parts[j] += 1
             if parts[j] == 4:
-                yv[j, :, wide] = acc[j, :, wide].astype(yv.dtype)
-                y_out(j).start()
+                yv[j, :, wide] = acc[j, yrow(1 - pi), wide].astype(yv.dtype)
+                y_ref[layout[j][0], :, cols(j, nu)] = acc[j, yrow(pi), wide].astype(y_ref.dtype)
 
     for name in names:
         if name not in received:
             remote(name, True).wait_recv()
     for name in names:
         remote(name).wait_send()
-    for j in range(chunks):
-        y_out(j).wait()
 
 
 def solution(mesh):
@@ -360,22 +363,22 @@
         any_spec = pl.BlockSpec(memory_space=pl.ANY)
         y, _ = pl.pallas_call(
             functools.partial(body, prog, tasks, names, modes, dims),
-            out_shape=(jax.ShapeDtypeStruct(x.shape, x.dtype), jax.ShapeDtypeStruct((chunks, 4, kb, width), x.dtype)),
+            out_shape=(pltpu.VMEM(x.shape, x.dtype), jax.ShapeDtypeStruct((chunks, 4, kb, width), x.dtype)),
             in_specs=[any_spec, any_spec],
-            out_specs=(any_spec, any_spec),
+            out_specs=(pl.BlockSpec(memory_space=pltpu.VMEM), any_spec),
             scratch_shapes=[
                 pltpu.VMEM((4, 2 * s, kb), a.dtype),
                 pltpu.VMEM((SLOTS, kb, width), x.dtype),
+                pltpu.VMEM((4, kb, layout[-1][2]), x.dtype),
                 pltpu.VMEM((chunks, s, width), x.dtype),
-                pltpu.VMEM((chunks, 2 * s, width), x.dtype),
+                pltpu.VMEM((chunks, s, width), x.dtype),
                 pltpu.VMEM((chunks, 2 * s, width), jnp.float32),
                 pltpu.SemaphoreType.DMA((len(names),)),
                 pltpu.SemaphoreType.DMA((len(names),)),
                 pltpu.SemaphoreType.DMA((2 * chunks + 1,)),
-                pltpu.SemaphoreType.DMA((chunks,)),
                 pltpu.SemaphoreType.DMA((SLOTS,)),
             ],
-            compiler_params=pltpu.CompilerParams(collective_id=0, has_side_effects=True, vmem_limit_bytes=60 * 1024 * 1024),
+            compiler_params=pltpu.CompilerParams(collective_id=0, has_side_effects=True, vmem_limit_bytes=54 * 1024 * 1024),
         )(a, x)
         return y
 

time: 275 us -> 272 us (0.989)
  local copies, waits for them, and re-layouts: 5.24 us -> 2.19 us
    unnamed x1, local copies, waits for them, and re-layouts: 5.24 us -> 2.19 us
where the time goes in v4:
time: 272 us
  Pallas kernels  270 us (99%)
    pallas_call x1, Pallas kernels, local(): pl.pallas_call(functools.partial(body, prog, tasks, names, modes, dims),...  270 us

profile of v4, /device:TPU:0, one launch (start us, length us, event | category | flops | bytes accessed | tf_op | source)
XLA Modules:
  0.0 271.9 jit_solution(8736093391024172628)
XLA Ops:
  0.0 269.7 %shard_map.28 = (bf16[3,384,2048]{2,1,0:T(8,128)(2,1)S(1)}, bf16[13,4,3072,256]{3,2,1,0:T(8,128)(2,1)}) custom-call(bf16[384,3072]{1,0:T(8,128)(2,1)} %a_ref.1, bf16[3,384,2048]{2,1,0:T(8,128)(2,1)} %x_ref.1), custom_call_target="tpu_custom_call" | custom-call | tf_op jit(solution)/shard_map/pallas_call | solution.py:364
  269.7 2.2 copy.4

commit v5 on v4

--- a/solution.py
+++ b/solution.py
@@ -8,15 +8,15 @@
 from jax.sharding import PartitionSpec as P
 
 MESH = pl.DeviceIdType.MESH
-MODES = "abbabbaabbabb"
+MODES = "babbabaababbb"
 A_PIECES = 4
 SLOTS = 5
 DEPTH_Q = 3
-TAIL_CHUNKS = 2
+TAIL_CHUNKS = 4
 MARGIN = 2.0
-PLAN_LAT = 2.5
-BLOCK_US = 1.8
-RATE = {"xp": 46.0e3, "xm": 46.0e3, "yp": 46.0e3, "ym": 46.0e3, "zl": 46.0e3, "zh": 46.0e3, "dd": 200.0e3}
+PLAN_LAT = 4.5
+BLOCK_US = 1.6
+RATE = {"xp": 46.0e3, "xm": 46.0e3, "yp": 46.0e3, "ym": 46.0e3, "zl": 46.0e3, "zh": 46.0e3, "dd": 300.0e3}
 LAT = {"dd": 2.5}
 
 

time: 272 us -> 266 us (0.978)
  Pallas kernels: 270 us -> 263 us
    pallas_call x1, Pallas kernels: 270 us -> 263 us  [local(): pl.pallas_call(functools.partial(body, prog, tasks, names, modes, dims),...]
where the time goes in v5:
time: 266 us; the launch traced here: 265 us
  Pallas kernels  263 us (99%)
    pallas_call x1, Pallas kernels, local(): pl.pallas_call(functools.partial(body, prog, tasks, names, modes, dims),...  263 us

profile of v5, /device:TPU:0, one launch (start us, length us, event | category | flops | bytes accessed | tf_op | source)
XLA Modules:
  0.0 265.3 jit_solution(9199342079660430709)
XLA Ops:
  0.0 263.1 %shard_map.28 = (bf16[3,384,2048]{2,1,0:T(8,128)(2,1)S(1)}, bf16[13,4,3072,256]{3,2,1,0:T(8,128)(2,1)}) custom-call(bf16[384,3072]{1,0:T(8,128)(2,1)} %a_ref.1, bf16[3,384,2048]{2,1,0:T(8,128)(2,1)} %x_ref.1), custom_call_target="tpu_custom_call" | custom-call | tf_op jit(solution)/shard_map/pallas_call | solution.py:364
  263.1 2.2 copy.4

commit v6 on v5

--- a/solution.py
+++ b/solution.py
@@ -14,10 +14,12 @@
 DEPTH_Q = 3
 TAIL_CHUNKS = 4
 MARGIN = 2.0
-PLAN_LAT = 4.5
+PLAN_LAT = 3.5
 BLOCK_US = 1.6
 RATE = {"xp": 46.0e3, "xm": 46.0e3, "yp": 46.0e3, "ym": 46.0e3, "zl": 46.0e3, "zh": 46.0e3, "dd": 300.0e3}
 LAT = {"dd": 2.5}
+WHOLE_K = 8
+KEYS = (-9.0, -1.5, -0.6, 1.2)
 
 
 def make_plan(units, modes, a_unit, block_us):
@@ -31,16 +33,38 @@
     for j in range(chunks):
         S, L, unit = ("S", j), ("L", j), units[j]
         add(L, "zl", unit, [], j - 1)
-        if modes[j] == "b":
-            add(("H", j, 0), "zh", unit, [], j - 1.5)
-            add(("H", j, 1), "zh", unit, [L], j - 1.5)
+        if modes[j] in "bc":
+            add(("H", j, 0), "zh", unit, [], j + KEYS[0])
+            add(("H", j, 1), "zh", unit, [L], j + KEYS[0])
             h = [("H", j, 0), ("H", j, 1)]
             for way, link in (("R", "xp"), ("L", "xm")):
-                add((way + "1", j, 0), link, 2 * unit, [S, L], (j, 1))
-                add((way + "1", j, 1), link, 2 * unit, h, (j, 1))
-            add(("R2", j), "xp", 2 * unit, [("R1", j, 0)], (j, 0))
-            add(("L2", j), "xm", 2 * unit, [("L1", j, 1)], (j, 0))
-            got = {0: [S, L] + h, -1: [("R1", j, 0), ("R1", j, 1)], 1: [("L1", j, 0), ("L1", j, 1)], 2: [("R2", j), ("L2", j)]}
+                add((way + "1", j, 0), link, 2 * unit, [S, L], (j + KEYS[2], 1))
+                add((way + "1", j, 1), link, 2 * unit, h, (j + KEYS[2], 1))
+            far = [("R2", j), ("L2", j)]
+            if modes[j] == "b":
+                add(far[0], "xp", 2 * unit, [("R1", j, 0)], (j + KEYS[3], 0))
+                add(far[1], "xm", 2 * unit, [("L1", j, 1)], (j + KEYS[3], 0))
+            else:
+                add(far[0], "xp", unit, [("R1", j, 0)], (j + KEYS[3], 0))
+                add(far[1], "xm", unit, [("L1", j, 0)], (j + KEYS[3], 0))
+                add(("H", j, 2), "zh", 2 * unit, far, j + KEYS[1])
+                far = far + [("H", j, 2)]
+            got = {0: [S, L] + h, -1: [("R1", j, 0), ("R1", j, 1)], 1: [("L1", j, 0), ("L1", j, 1)], 2: far}
+        elif modes[j] == "m":
+            add(("H", j, 9), "zh", unit, [L], j + KEYS[0])
+            for way, link in (("R", "xp"), ("L", "xm")):
+                add((way + "1", j, 0), link, unit, [], (j, 1))
+                add((way + "1", j, 1), link, unit, [L], (j, 1))
+                add((way + "1", j, 2), link, unit, [("H", j, 9)], (j, 1))
+                add((way + "3", j), link, unit // 2, [(way + "1", j, 2)], (j, 0))
+            add(("R2", j), "xp", unit, [("R1", j, 0)], (j, 0))
+            add(("L2", j), "xm", unit, [("L1", j, 1)], (j, 0))
+            for d, dep in ((0, S), (-1, ("R1", j, 0)), (1, ("L1", j, 0)), (2, ("R2", j))):
+                add(("H", j, d), "zh", unit, [dep], j + KEYS[1])
+            got = {0: [S, L, ("H", j, 9)], -1: [("R1", j, k) for k in range(3)], 1: [("L1", j, k) for k in range(3)],
+                   2: [("R2", j), ("L2", j), ("R3", j), ("L3", j)]}
+            for d in got:
+                got[d] = got[d] + [("H", j, d)]
         else:
             for way, link in (("R", "xp"), ("L", "xm")):
                 add((way + "1", j, 0), link, unit, [], (j, 1))
@@ -50,7 +74,7 @@
             pre = {0: [S, L], -1: [("R1", j, 0), ("R1", j, 1)], 1: [("L1", j, 0), ("L1", j, 1)], 2: [("R2", j), ("L2", j)]}
             got = {}
             for d in (0, -1, 1, 2):
-                add(("H", j, d), "zh", 2 * unit, pre[d], j)
+                add(("H", j, d), "zh", 2 * unit, pre[d], j + KEYS[1])
                 got[d] = pre[d] + [("H", j, d)]
         for d in (0, -1, 1, 2):
             add(("D", j, d), "dd", 4 * unit, got[d], j)
@@ -235,22 +259,30 @@
             return ref, ref, "dd"
         own, pair, other = krow(c, z, 1), krow(c, 2 * zh, 2), krow(c, 2 * (1 - zh), 2)
         if kind == "H":
-            if modes[j] == "b":
+            if modes[j] in "bc" and name[2] != 2:
                 at = z if name[2] == 0 else zl_peer
                 ref = xgat(j, x, krow(c, 3 - at if recv else at, 1))
                 return (xin(j, nu) if name[2] == 0 and not recv else ref), ref, "zh"
+            if modes[j] == "m":
+                at, block = (zl_peer, x) if name[2] == 9 else (z, xat(name[2]))
+                ref = xgat(j, block, krow(c, 3 - at if recv else at, 1))
+                return ref, ref, "zh"
             ref = xgat(j, xat(name[2]), other if recv else pair)
             return ref, ref, "zh"
         right = kind[0] == "R"
         link = "xp" if right else "xm"
         step = (-1 if right else 1) if recv else 0
-        if modes[j] == "b":
+        if modes[j] == "b" or (modes[j] == "c" and kind[1] == "1"):
             parts = (pair, other)
         else:
-            parts = (own, krow(c, zl_peer, 1))
+            parts = (own, krow(c, zl_peer, 1), krow(c, 3 - zl_peer, 1))
+        if kind[1] == "3":
+            at = (4 * c + 3 - zl_peer) * s + (0 if right else s // 2)
+            ref = xgat(j, xat(step + (-1 if right else 1)), pl.ds(pl.multiple_of(at, 16), s // 2))
+            return ref, ref, link
         if kind[1] == "1":
             ref = xgat(j, xat(step), parts[name[2]])
-            direct = modes[j] == "a" and name[2] == 0 and not recv
+            direct = modes[j] in "am" and name[2] == 0 and not recv
             return (xin(j, nu) if direct else ref), ref, link
         ref = xgat(j, xat(step + (-1 if right else 1)), parts[0 if right else 1])
         return ref, ref, link
@@ -299,7 +331,8 @@
     parts = [0] * chunks
     for op, what in prog:
         if op == "start":
-            remote(what).start()
+            if what != ("Y", tasks[-1][0]):
+                remote(what).start()
         elif op == "load":
             if tasks[what][0] < chunks - 1:
                 load(what).start()
@@ -326,13 +359,28 @@
             def rhs(lanes, slot=slot, block=block, j=j, wide=wide):
                 return xt[block, lanes, :] if j == chunks - 1 else xv[slot, lanes, wide]
 
-            def step(k, carry, rhs=rhs, block=block, j=j, wide=wide):
-                lanes = pl.ds(pl.multiple_of(k * kk, 128), kk)
-                acc[j, :, wide] += jnp.dot(av[block, :, lanes], rhs(lanes), preferred_element_type=jnp.float32)
-                return carry
-
-            lax.fori_loop(0, kb // kk, step, 0)
+            whole = what == len(tasks) - 1 or (what >= len(tasks) - WHOLE_K and layout[j][2] == 256)
+            deep = kb if whole else kk
+
+            def step(k, rows, rhs=rhs, block=block, j=j, wide=wide, deep=deep):
+                lanes = slice(None) if deep == kb else pl.ds(pl.multiple_of(k * deep, 128), deep)
+                acc[j, rows, wide] += jnp.dot(av[block, rows, lanes], rhs(lanes), preferred_element_type=jnp.float32)
+
+            def loop(rows, step=step, deep=deep):
+                if deep == kb:
+                    step(0, rows)
+                else:
+                    lax.fori_loop(0, kb // deep, lambda k, carry: (step(k, rows), carry)[1], 0)
+
             parts[j] += 1
+            if what == len(tasks) - 1:
+                loop(yrow(1 - pi))
+                yv[j, :, wide] = acc[j, yrow(1 - pi), wide].astype(yv.dtype)
+                remote(("Y", j)).start()
+                loop(yrow(pi))
+                y_ref[layout[j][0], :, cols(j, nu)] = acc[j, yrow(pi), wide].astype(y_ref.dtype)
+                continue
+            loop(slice(None))
             if parts[j] == 4:
                 yv[j, :, wide] = acc[j, yrow(1 - pi), wide].astype(yv.dtype)
                 y_ref[layout[j][0], :, cols(j, nu)] = acc[j, yrow(pi), wide].astype(y_ref.dtype)

time: 266 us -> 267 us (level)
  no operation moved by 1% of the time
where the time goes in v6:
time: 267 us
  Pallas kernels  265 us (99%)
    pallas_call x1, Pallas kernels, local(): pl.pallas_call(functools.partial(body, prog, tasks, names, modes, dims),...  265 us

profile of v6, /device:TPU:0, one launch (start us, length us, event | category | flops | bytes accessed | tf_op | source)
XLA Modules:
  0.0 267.0 jit_solution(13489919456133520320)
XLA Ops:
  0.0 264.8 %shard_map.28 = (bf16[3,384,2048]{2,1,0:T(8,128)(2,1)S(1)}, bf16[13,4,3072,256]{3,2,1,0:T(8,128)(2,1)}) custom-call(bf16[384,3072]{1,0:T(8,128)(2,1)} %a_ref.1, bf16[3,384,2048]{2,1,0:T(8,128)(2,1)} %x_ref.1), custom_call_target="tpu_custom_call" | custom-call | tf_op jit(solution)/shard_map/pallas_call | solution.py:412
  264.8 2.2 copy.4

commit v7 on v6

--- a/solution.py
+++ b/solution.py
@@ -14,12 +14,12 @@
 DEPTH_Q = 3
 TAIL_CHUNKS = 4
 MARGIN = 2.0
-PLAN_LAT = 3.5
+PLAN_LAT = 4.5
 BLOCK_US = 1.6
 RATE = {"xp": 46.0e3, "xm": 46.0e3, "yp": 46.0e3, "ym": 46.0e3, "zl": 46.0e3, "zh": 46.0e3, "dd": 300.0e3}
 LAT = {"dd": 2.5}
 WHOLE_K = 8
-KEYS = (-9.0, -1.5, -0.6, 1.2)
+KEYS = (-1.5, 0.0, 0.0, 0.0)
 
 
 def make_plan(units, modes, a_unit, block_us):

time: 267 us -> 266 us (level)
  no operation moved by 1% of the time
where the time goes in v7:
time: 266 us
  Pallas kernels  264 us (99%)
    pallas_call x1, Pallas kernels, local(): pl.pallas_call(functools.partial(body, prog, tasks, names, modes, dims),...  264 us

profile of v7, /device:TPU:0, one launch (start us, length us, event | category | flops | bytes accessed | tf_op | source)
XLA Modules:
  0.0 266.1 jit_solution(8546522003586971651)
XLA Ops:
  0.0 263.9 %shard_map.28 = (bf16[3,384,2048]{2,1,0:T(8,128)(2,1)S(1)}, bf16[13,4,3072,256]{3,2,1,0:T(8,128)(2,1)}) custom-call(bf16[384,3072]{1,0:T(8,128)(2,1)} %a_ref.1, bf16[3,384,2048]{2,1,0:T(8,128)(2,1)} %x_ref.1), custom_call_target="tpu_custom_call" | custom-call | tf_op jit(solution)/shard_map/pallas_call | solution.py:412
  263.9 2.2 copy.4

commit v8 on v7

--- a/solution.py
+++ b/solution.py
@@ -8,18 +8,18 @@
 from jax.sharding import PartitionSpec as P
 
 MESH = pl.DeviceIdType.MESH
-MODES = "babbabaababbb"
+MODES = "abbababmabacbb"
 A_PIECES = 4
 SLOTS = 5
 DEPTH_Q = 3
-TAIL_CHUNKS = 4
-MARGIN = 2.0
+TAIL_CHUNKS = 6
+MARGIN = 0.5
 PLAN_LAT = 4.5
 BLOCK_US = 1.6
 RATE = {"xp": 46.0e3, "xm": 46.0e3, "yp": 46.0e3, "ym": 46.0e3, "zl": 46.0e3, "zh": 46.0e3, "dd": 300.0e3}
 LAT = {"dd": 2.5}
-WHOLE_K = 8
-KEYS = (-1.5, 0.0, 0.0, 0.0)
+NEAR = 2
+KEYS = (-9.0, -1.5, 0.6, 1.2)
 
 
 def make_plan(units, modes, a_unit, block_us):
@@ -153,7 +153,7 @@
                 settle(task[3])
                 settle(task[4])
                 prog.append(("load", len(tasks)))
-                ready_at[len(tasks)] = t + 1.7 if task[0] < chunks - 1 else t
+                ready_at[len(tasks)] = t + 1.7 if task[0] < chunks - NEAR else t
                 tasks.append(task[:3])
                 continue
         if computed < len(tasks) and ready_at[computed] <= t:
@@ -181,6 +181,7 @@
 def body(prog, tasks, names, modes, dims, a_ref, x_ref, y_ref, xg, av, xv, xt, xs, yv, acc, ssem, rsem, lsem, vsem):
     layout, s, kb, half, kk = dims
     chunks = len(layout)
+    near = chunks - NEAR
     z, y, i = lax.axis_index("depth"), lax.axis_index("col"), lax.axis_index("row")
     x, c = i // 2, i % 2
     zh, pi = z // 2, z % 2
@@ -214,8 +215,8 @@
         return x_ref.at[layout[j][0], :, cols(j, part)]
 
     def xgat(j, block, rows):
-        if j == chunks - 1:
-            return xt.at[block, rows]
+        if j >= near:
+            return xt.at[j - near, block, rows]
         return xg.at[j, block, rows, lane(j)]
 
     rows_a = s // A_PIECES
@@ -296,7 +297,7 @@
             device_id=dev[link], device_id_type=MESH)
 
     def stage_in(j):
-        dst = xgat(j, x, krow(c, z, 1)) if j == chunks - 1 else xs.at[j, :, lane(j)]
+        dst = xgat(j, x, krow(c, z, 1)) if j >= near else xs.at[j, :, lane(j)]
         return pltpu.make_async_copy(xin(j, nu), dst, lsem.at[j])
 
     def stage_out(j):
@@ -322,7 +323,7 @@
     staged = [False]
 
     def finish_stage():
-        for j in range(chunks - 1):
+        for j in range(near):
             stage_in(j).wait()
             stage_out(j).start()
         staged[0] = True
@@ -331,16 +332,15 @@
     parts = [0] * chunks
     for op, what in prog:
         if op == "start":
-            if what != ("Y", tasks[-1][0]):
-                remote(what).start()
+            remote(what).start()
         elif op == "load":
-            if tasks[what][0] < chunks - 1:
+            if tasks[what][0] < near:
                 load(what).start()
         elif op == "wait":
             if not staged[0]:
                 finish_stage()
             if what[0] == "S":
-                (stage_in if what[1] == chunks - 1 else stage_out)(what[1]).wait()
+                (stage_in if what[1] >= near else stage_out)(what[1]).wait()
             elif what[0] == "AS":
                 a_in().wait()
             else:
@@ -350,37 +350,22 @@
             j, axis, e = tasks[what]
             slot = what % SLOTS
             wide = lane(j)
-            if j < chunks - 1:
+            if j < near:
                 load(what).wait()
             if parts[j] == 0:
                 acc[j, :, wide] = jnp.zeros((2 * s, layout[j][2]), jnp.float32)
             block = yat(e) if axis == "y" else xat(e)
 
             def rhs(lanes, slot=slot, block=block, j=j, wide=wide):
-                return xt[block, lanes, :] if j == chunks - 1 else xv[slot, lanes, wide]
-
-            whole = what == len(tasks) - 1 or (what >= len(tasks) - WHOLE_K and layout[j][2] == 256)
-            deep = kb if whole else kk
-
-            def step(k, rows, rhs=rhs, block=block, j=j, wide=wide, deep=deep):
-                lanes = slice(None) if deep == kb else pl.ds(pl.multiple_of(k * deep, 128), deep)
-                acc[j, rows, wide] += jnp.dot(av[block, rows, lanes], rhs(lanes), preferred_element_type=jnp.float32)
-
-            def loop(rows, step=step, deep=deep):
-                if deep == kb:
-                    step(0, rows)
-                else:
-                    lax.fori_loop(0, kb // deep, lambda k, carry: (step(k, rows), carry)[1], 0)
-
+                return xt[j - near, block, lanes, :] if j >= near else xv[slot, lanes, wide]
+
+            def step(k, carry, rhs=rhs, block=block, j=j, wide=wide):
+                lanes = pl.ds(pl.multiple_of(k * kk, 128), kk)
+                acc[j, :, wide] += jnp.dot(av[block, :, lanes], rhs(lanes), preferred_element_type=jnp.float32)
+                return carry
+
+            lax.fori_loop(0, kb // kk, step, 0)
             parts[j] += 1
-            if what == len(tasks) - 1:
-                loop(yrow(1 - pi))
-                yv[j, :, wide] = acc[j, yrow(1 - pi), wide].astype(yv.dtype)
-                remote(("Y", j)).start()
-                loop(yrow(pi))
-                y_ref[layout[j][0], :, cols(j, nu)] = acc[j, yrow(pi), wide].astype(y_ref.dtype)
-                continue
-            loop(slice(None))
             if parts[j] == 4:
                 yv[j, :, wide] = acc[j, yrow(1 - pi), wide].astype(yv.dtype)
                 y_ref[layout[j][0], :, cols(j, nu)] = acc[j, yrow(pi), wide].astype(y_ref.dtype)
@@ -400,8 +385,8 @@
         width = 256 if half % 256 == 0 else 128
         layout = [(r, at, width) for r in range(rhs) for at in range(0, half, width)]
         if width == 256:
-            r, at, _ = layout.pop()
-            layout += [(r, at, 128), (r, at + 128, 128)]
+            split = layout[-2:]
+            layout = layout[:-2] + [(r, at + more, 128) for r, at, _ in split for more in (0, 128)]
         chunks = len(layout)
         modes = (MODES * chunks)[:chunks]
         kk = 1024 if kb % 1024 == 0 else 256
@@ -417,7 +402,7 @@
             scratch_shapes=[
                 pltpu.VMEM((4, 2 * s, kb), a.dtype),
                 pltpu.VMEM((SLOTS, kb, width), x.dtype),
-                pltpu.VMEM((4, kb, layout[-1][2]), x.dtype),
+                pltpu.VMEM((NEAR, 4, kb, layout[-1][2]), x.dtype),
                 pltpu.VMEM((chunks, s, width), x.dtype),
                 pltpu.VMEM((chunks, s, width), x.dtype),
                 pltpu.VMEM((chunks, 2 * s, width), jnp.float32),

time: 266 us -> 264 us (level)
  Pallas kernels: 264 us -> 261 us
    pallas_call x1, Pallas kernels: 264 us -> 261 us  [local(): pl.pallas_call(functools.partial(body, prog, tasks, names, modes, dims),...]
where the time goes in v8:
time: 264 us; the launch traced here: 263 us
  Pallas kernels  261 us (99%)
    pallas_call x1, Pallas kernels, local(): pl.pallas_call(functools.partial(body, prog, tasks, names, modes, dims),...  261 us

profile of v8, /device:TPU:0, one launch (start us, length us, event | category | flops | bytes accessed | tf_op | source)
XLA Modules:
  0.0 263.3 jit_solution(2177108313829874380)
XLA Ops:
  0.0 261.1 %shard_map.28 = (bf16[3,384,2048]{2,1,0:T(8,128)(2,1)S(1)}, bf16[14,4,3072,256]{3,2,1,0:T(8,128)(2,1)}) custom-call(bf16[384,3072]{1,0:T(8,128)(2,1)} %a_ref.1, bf16[3,384,2048]{2,1,0:T(8,128)(2,1)} %x_ref.1), custom_call_target="tpu_custom_call" | custom-call | tf_op jit(solution)/shard_map/pallas_call | solution.py:397
  261.1 2.2 copy.4

commit v9 on v8

--- a/solution.py
+++ b/solution.py
@@ -8,18 +8,18 @@
 from jax.sharding import PartitionSpec as P
 
 MESH = pl.DeviceIdType.MESH
-MODES = "abbababmabacbb"
+MODES = "abbmbaababacbb"
 A_PIECES = 4
 SLOTS = 5
 DEPTH_Q = 3
-TAIL_CHUNKS = 6
-MARGIN = 0.5
-PLAN_LAT = 4.5
+TAIL_CHUNKS = 5
+MARGIN = 2.0
+PLAN_LAT = 5.0
 BLOCK_US = 1.6
 RATE = {"xp": 46.0e3, "xm": 46.0e3, "yp": 46.0e3, "ym": 46.0e3, "zl": 46.0e3, "zh": 46.0e3, "dd": 300.0e3}
 LAT = {"dd": 2.5}
 NEAR = 2
-KEYS = (-9.0, -1.5, 0.6, 1.2)
+KEYS = (-3.0, 1.5, 0.6, 1.2)
 
 
 def make_plan(units, modes, a_unit, block_us):

time: 264 us -> 266 us (level)
  Pallas kernels: 261 us -> 264 us
where the time goes in v9:
time: 266 us
  Pallas kernels  264 us (99%)
    pallas_call x1, Pallas kernels, local(): pl.pallas_call(functools.partial(body, prog, tasks, names, modes, dims),...  264 us

profile of v9, /device:TPU:0, one launch (start us, length us, event | category | flops | bytes accessed | tf_op | source)
XLA Modules:
  0.0 265.7 jit_solution(6371609753692861116)
XLA Ops:
  0.0 263.5 %shard_map.28 = (bf16[3,384,2048]{2,1,0:T(8,128)(2,1)S(1)}, bf16[14,4,3072,256]{3,2,1,0:T(8,128)(2,1)}) custom-call(bf16[384,3072]{1,0:T(8,128)(2,1)} %a_ref.1, bf16[3,384,2048]{2,1,0:T(8,128)(2,1)} %x_ref.1), custom_call_target="tpu_custom_call" | custom-call | tf_op jit(solution)/shard_map/pallas_call | solution.py:397
  263.5 2.2 copy.4
